TPU v7x, 8 devices: a whole 2x2x1 slice. The times are simulated.
8 devices in a mesh: dp: 1 (over z), row: 2 (over y), co: 2 (over x), ci: 2 (over core).
Axes of the slice: x: 2, y: 2, z: 1, core: 2. Of those that a mesh axis runs over, the one named last changes fastest.
Arguments:
- x_in: bfloat16 [4096, 4096], P(('dp', 'row'), ('co', 'ci'))
- w_up: bfloat16 [4096, 14336], P('row', ('co', 'ci'))
- w_down: bfloat16 [14336, 4096], P('row', ('co', 'ci'))
Outputs:
- output: bfloat16 [4096, 4096], P(('dp', 'row'), ('co', 'ci'))
All inputs are finite; a program needn't handle non-finite values.
Results may differ from a plain program's by a relative error of at most 0.001.
Values are sent between devices in bfloat16 or wider.
A program may use at most 1 GiB of HBM per device.

v0:
```python
import jax
import jax.numpy as jnp
from jax import lax
from jax.sharding import PartitionSpec as P, NamedSharding

ROW_AXES = ("dp", "row")
COL_AXES = ("co", "ci")


def solution(mesh):
    def local_mlp(x_blk, w_up_blk, w_down_blk):
        x_rows = lax.all_gather(x_blk, COL_AXES, axis=1, tiled=True)
        w_up_cols = lax.all_gather(w_up_blk, "row", axis=0, tiled=True)
        pre_act = jnp.dot(x_rows, w_up_cols, preferred_element_type=jnp.float32)
        hidden = jax.nn.gelu(pre_act, approximate=True).astype(jnp.bfloat16)
        h_rows = lax.all_gather(hidden, COL_AXES, axis=1, tiled=True)
        w_down_cols = lax.all_gather(w_down_blk, "row", axis=0, tiled=True)
        return jnp.dot(h_rows, w_down_cols, preferred_element_type=jnp.float32).astype(jnp.bfloat16)

    act_spec = P(ROW_AXES, COL_AXES)
    wgt_spec = P("row", COL_AXES)
    return jax.shard_map(local_mlp, mesh=mesh, in_specs=(act_spec, wgt_spec, wgt_spec), out_specs=act_spec, check_vma=False)
```

profile of v0, /device:TPU:0, one launch (start us, length us, event | category | flops | bytes accessed | tf_op | source)
XLA Modules:
  0.0 1218.3 jit_solution(8050259787874468232)
XLA Ops:
  6.5 0.0 all-gather.5.cloned.1.call-start
  6.5 0.7 all-gather.5.cloned.1.call-update
  7.3 0.0 all-gather.7.cloned.1.call-start
  7.3 0.7 all-gather.7.cloned.1.call-update
  8.0 0.0 all-gather.11.cloned.1.call-start
  8.1 0.7 all-gather.11.cloned.1.call-update
  8.7 0.0 all-gather.9.cloned.1.call-start
  8.8 107.1 %all-gather.5.cloned.1.call-done = bf16[2048,4096]{1,0:T(8,128)(2,1)} async-done(((bf16[2048,1024]{1,0:T(8,128)(2,1)}), bf16[2048,4096]{1,0:T(8,128)(2,1)}) %all-gather.5.cloned.1.call-update) | async-done | bytes 16777232 | tf_op jit(solution)/shard_map/all_gather | solution.py:12
  115.9 340.9 %all-gather.7.cloned.1.call-done = bf16[4096,3584]{1,0:T(8,128)(2,1)} async-done(((bf16[2048,3584]{1,0:T(8,128)(2,1)}), bf16[4096,3584]{1,0:T(8,128)(2,1)}) %all-gather.7.cloned.1.call-update) | async-done | bytes 29360144 | tf_op jit(solution)/shard_map/all_gather | solution.py:13
  456.8 77.8 %fusion.7 = bf16[2048,3584]{1,0:T(8,128)(2,1)} fusion(bf16[2048,4096]{1,0:T(8,128)(2,1)} %all-gather.5.cloned.1.call-done, bf16[4096,3584]{1,0:T(8,128)(2,1)} %all-gather.7.cloned.1.call-done), kind=kOutput, calls=%fused_computation.8 | convolution fusion | flops 60195602432 | bytes 60817408 | tf_op jit(solution)/shard_map/dot_general | solution.py:14
  534.7 0.0 all-gather.9.cloned.1.call-update
  534.7 263.1 %all-gather.11.cloned.1.call-done = bf16[14336,1024]{1,0:T(8,128)(2,1)} async-done(((bf16[7168,1024]{1,0:T(8,128)(2,1)}), bf16[14336,1024]{1,0:T(8,128)(2,1)}) %all-gather.11.cloned.1.call-update) | async-done | bytes 29360144 | tf_op jit(solution)/shard_map/all_gather | solution.py:17
  797.8 344.6 %all-gather.9.cloned.1.call-done = bf16[2048,14336]{1,0:T(8,128)(2,1)} async-done(((bf16[2048,3584]{1,0:T(8,128)(2,1)}), bf16[2048,14336]{1,0:T(8,128)(2,1)}) %all-gather.9.cloned.1.call-update) | async-done | bytes 58720272 | tf_op jit(solution)/shard_map/all_gather | solution.py:16
  1142.4 69.4 %convolution_convert_fusion = bf16[2048,1024]{1,0:T(8,128)(2,1)} fusion(bf16[2048,14336]{1,0:T(8,128)(2,1)} %all-gather.9.cloned.1.call-done, bf16[14336,1024]{1,0:T(8,128)(2,1)} %all-gather.11.cloned.1.call-done), kind=kOutput, calls=%fused_computation.9 | convolution fusion | flops 60131639296 | bytes 92274688 | tf_op jit(solution)/shard_map/dot_general | solution.py:18
Async XLA Ops:
  6.5 109.4 %all-gather.5.cloned.1.call-start = ((), (), s32[]{:S(2)}) async-start(), calls=%async_computation | async-start | bytes 20971520 | tf_op jit(solution)/shard_map/all_gather | solution.py:12
  7.3 449.6 %all-gather.7.cloned.1.call-start = ((), (), s32[]{:S(2)}) async-start(), calls=%async_computation.1 | async-start | bytes 44040192 | tf_op jit(solution)/shard_map/all_gather | solution.py:13
  8.0 789.8 %all-gather.11.cloned.1.call-start = ((), (), s32[]{:S(2)}) async-start(), calls=%async_computation.3 | async-start | bytes 44040192 | tf_op jit(solution)/shard_map/all_gather | solution.py:17
  8.7 1133.6 %all-gather.9.cloned.1.call-start = ((), (), s32[]{:S(2)}) async-start(), calls=%async_computation.2 | async-start | bytes 73400320 | tf_op jit(solution)/shard_map/all_gather | solution.py:16
Sparse Core Ops, SparseCore 0:
  8.9 107.0 all-gather.4
  117.4 339.3 all-gather.6
  458.4 339.3 all-gather.10
  799.2 343.1 all-gather.8
where the time goes:
time: 1220 us
  waiting for transfers between devices  1060 us (87%)
  matrix products  147 us (12%)
  between operations  13.1 us (1%)
    all_gather x1, waiting for transfers between devices, local_mlp(): h_rows = lax.all_gather(hidden, COL_AXES, axis=1, tiled=True)  345 us
    all_gather x1, waiting for transfers between devices, local_mlp(): w_up_cols = lax.all_gather(w_up_blk, 'row', axis=0, tiled=True)  341 us
    all_gather x1, waiting for transfers between devices, local_mlp(): w_down_cols = lax.all_gather(w_down_blk, 'row', axis=0, tiled=True)  263 us
    all_gather x1, waiting for transfers between devices, local_mlp(): x_rows = lax.all_gather(x_blk, COL_AXES, axis=1, tiled=True)  107 us
    dot_general x1, matrix products, local_mlp(): pre_act = jnp.dot(x_rows, w_up_cols, preferred_element_type=jnp.float32)  77.8 us
    dot_general x1, matrix products, local_mlp(): jnp.dot(h_rows, w_down_cols, preferred_element_type=jnp.float32)  69.4 us
  transfers between devices with their start and end apart: 4, of which 4 were waited for; matrix products, arithmetic and copies ran while one was open for 6% of the time, Pallas kernels for 0%

commit v1 on v0

v1 whole, which is shorter than its diff:
```python
import functools
import math

import jax
import jax.numpy as jnp
from jax import lax
from jax.experimental import pallas as pl
from jax.experimental.pallas import tpu as pltpu
from jax.sharding import PartitionSpec as P

ROW_AXES = ("dp", "row")
COL_AXES = ("co", "ci")
MESH = pl.DeviceIdType.MESH
FC = 512
TM = 256
GELU_C = math.sqrt(2.0 / math.pi)


def gelu(p):
    return 0.5 * p * (1.0 + jnp.tanh(GELU_C * (p + 0.044715 * (p * p * p))))


def kernel(x, w1, w2, y, w1p, hq, xv, wv, hv, hb, wb, w2p, acc, yv,
           s_w1, r_w1, s_w2, r_w2, s_x, r_x, s_hfar, r_hfar, s_hmate, r_hmate, s_fwd, r_fwd,
           s_hloc, s_ld, s_hb, s_wb, s_y):
    f32 = jnp.float32
    rows, kq = x.shape
    kh, fq = w1.shape
    n_up = fq // FC
    n_dn = w2.shape[0] // FC
    row, co, ci = lax.axis_index("row"), lax.axis_index("co"), lax.axis_index("ci")
    vert, far, mate = {"row": 1 - row}, {"co": 1 - co}, {"ci": 1 - ci}

    barrier = pltpu.get_barrier_semaphore()
    for dev in (vert, far, mate):
        pl.semaphore_signal(barrier, inc=1, device_id=dev, device_id_type=MESH)
    pl.semaphore_wait(barrier, 3)

    def rdma(src, dst, send, recv, dev):
        return pltpu.make_async_remote_copy(
            src_ref=src, dst_ref=dst, send_sem=send, recv_sem=recv, device_id=dev, device_id_type=MESH)

    def cols(i):
        return pl.ds(pl.multiple_of(i * FC, FC), FC)

    def w1_copy(i):
        return rdma(w1.at[:, cols(i)], w1p.at[:, cols(i)], s_w1.at[i], r_w1.at[i], vert)

    def w2_copy(i):
        return rdma(w2.at[cols(i)], w2p.at[cols(i)], s_w2.at[i], r_w2.at[i], vert)

    x_far = rdma(x, xv.at[co, ci], s_x.at[0], r_x.at[0], far)
    x_mate = rdma(x, xv.at[co, ci], s_x.at[1], r_x.at[1], mate)
    x_fwd = rdma(xv.at[1 - co, ci], xv.at[1 - co, ci], s_x.at[2], r_x.at[2], mate)
    x_own = pltpu.make_async_copy(x, xv.at[co, ci], s_ld.at[0])

    def start(copy):
        def body(i, c):
            copy(i).start()
            return c
        return body

    w1_copy(0).start()
    x_far.start()
    x_mate.start()
    x_own.start()
    lax.fori_loop(1, n_up, start(w1_copy), 0)
    lax.fori_loop(0, n_dn, start(w2_copy), 0)
    x_own.wait()
    x_mate.wait()
    x_far.wait()
    x_fwd.start()
    x_fwd.wait()

    def h_copies(i, slot):
        src = hv.at[slot]
        dst = hq.at[co, ci, :, cols(i)]
        return (rdma(src, dst, s_hfar.at[i], r_hfar.at[i], far),
                rdma(src, dst, s_hmate.at[i], r_hmate.at[i], mate),
                pltpu.make_async_copy(src, dst, s_hloc.at[slot]))

    def h_forward(i):
        blk = hq.at[1 - co, ci, :, cols(i)]
        return rdma(blk, blk, s_fwd.at[i], r_fwd.at[i], mate)

    def h_drain(i, slot):
        a, b, c = h_copies(i, slot)
        a.wait_send()
        b.wait_send()
        c.wait()

    def up(i, carry):
        slot = lax.rem(i, 2)
        own = pltpu.make_async_copy(w1.at[:, cols(i)], wv.at[row], s_ld.at[0])
        own.start()
        w1_copy(i).wait_recv()
        peer = pltpu.make_async_copy(w1p.at[:, cols(i)], wv.at[1 - row], s_ld.at[1])
        peer.start()

        @pl.when(i >= 2)
        def _():
            h_drain(i - 2, slot)
            a, _, _ = h_copies(i - 2, slot)
            a.wait_recv()
            h_forward(i - 2).start()

        own.wait()
        peer.wait()

        def tile(m, c):
            r = pl.ds(pl.multiple_of(m * TM, TM), TM)
            p = None
            for k in range(4):
                a, b = divmod(k, 2)
                t = jnp.dot(xv[a, b, r, :], wv[a, b * kq:(b + 1) * kq, :], preferred_element_type=f32)
                p = t if p is None else p + t
            hv[slot, r, :] = gelu(p).astype(jnp.bfloat16)
            return c

        lax.fori_loop(0, rows // TM, tile, 0)
        for c in h_copies(i, slot):
            c.start()
        return carry

    lax.fori_loop(0, n_up, up, 0)

    def tail(i, carry):
        slot = lax.rem(i, 2)
        h_drain(i, slot)
        a, _, _ = h_copies(i, slot)
        a.wait_recv()
        h_forward(i).start()
        return carry

    lax.fori_loop(n_up - 2, n_up, tail, 0)

    def settle(i, carry):
        _, b, _ = h_copies(i, lax.rem(i, 2))
        b.wait_recv()
        h_forward(i).wait()
        return carry

    lax.fori_loop(0, n_up, settle, 0)

    def h_load(t, side):
        return pltpu.make_async_copy(
            hq.at[side, t // n_up, :, cols(lax.rem(t, n_up))], hb.at[lax.rem(t, 2)], s_hb.at[lax.rem(t, 2)])

    def w2_load(t):
        return pltpu.make_async_copy(w2.at[cols(t)], wb.at[lax.rem(t, 2)], s_wb.at[lax.rem(t, 2)])

    acc[...] = jnp.zeros_like(acc)
    h_load(0, row).start()
    w2_load(0).start()

    def near(t, carry):
        slot = lax.rem(t, 2)

        @pl.when(t + 1 < n_dn)
        def _():
            h_load(t + 1, row).start()
            w2_load(t + 1).start()

        h_load(t, row).wait()
        w2_load(t).wait()

        def tile(m, c):
            r = pl.ds(pl.multiple_of(m * TM, TM), TM)
            acc[r, :] += jnp.dot(hb[slot, r, :], wb[slot], preferred_element_type=f32)
            return c

        lax.fori_loop(0, rows // TM, tile, 0)
        return carry

    lax.fori_loop(0, n_dn, near, 0)
    h_load(0, 1 - row).start()

    def away(t, carry):
        slot = lax.rem(t, 2)
        h_load(t + 1, 1 - row).start()
        h_load(t, 1 - row).wait()
        w2_copy(t).wait_recv()

        def tile(m, c):
            r = pl.ds(pl.multiple_of(m * TM, TM), TM)
            acc[r, :] += jnp.dot(hb[slot, r, :], w2p[cols(t), :], preferred_element_type=f32)
            return c

        lax.fori_loop(0, rows // TM, tile, 0)
        return carry

    lax.fori_loop(0, n_dn - 1, away, 0)

    t = n_dn - 1
    slot = t % 2
    h_load(t, 1 - row).wait()
    w2_copy(t).wait_recv()

    def y_copy(m):
        r = pl.ds(pl.multiple_of(m * TM, TM), TM)
        return pltpu.make_async_copy(yv.at[r], y.at[r], s_y.at[m])

    def last(m, c):
        r = pl.ds(pl.multiple_of(m * TM, TM), TM)
        out = acc[r, :] + jnp.dot(hb[slot, r, :], w2p[t * FC:(t + 1) * FC, :], preferred_element_type=f32)
        yv[r, :] = out.astype(jnp.bfloat16)
        y_copy(m).start()
        return c

    lax.fori_loop(0, rows // TM, last, 0)

    def w1_sent(i, c):
        w1_copy(i).wait_send()
        return c

    def w2_sent(i, c):
        w2_copy(i).wait_send()
        return c

    lax.fori_loop(0, n_up, w1_sent, 0)
    lax.fori_loop(0, n_dn, w2_sent, 0)

    def y_done(m, c):
        y_copy(m).wait()
        return c

    lax.fori_loop(0, rows // TM, y_done, 0)


def solution(mesh):
    def local_mlp(x, w1, w2):
        rows, kq = x.shape
        kh, fq = w1.shape
        fh, nq = w2.shape
        n_up, n_dn = fq // FC, fh // FC
        bf, f32 = jnp.bfloat16, jnp.float32
        hbm = pl.BlockSpec(memory_space=pltpu.HBM)
        dma = lambda n: pltpu.SemaphoreType.DMA((n,))
        outs = pl.pallas_call(
            kernel,
            name="mlp",
            out_shape=(
                jax.ShapeDtypeStruct((rows, nq), bf),
                jax.ShapeDtypeStruct((kh, fq), bf),
                jax.ShapeDtypeStruct((2, 2, rows, fq), bf),
            ),
            in_specs=[hbm] * 3,
            out_specs=(hbm,) * 3,
            scratch_shapes=[
                pltpu.VMEM((2, 2, rows, kq), bf),
                pltpu.VMEM((2, kh, FC), bf),
                pltpu.VMEM((2, rows, FC), bf),
                pltpu.VMEM((2, rows, FC), bf),
                pltpu.VMEM((2, FC, nq), bf),
                pltpu.VMEM((fh, nq), bf),
                pltpu.VMEM((rows, nq), f32),
                pltpu.VMEM((rows, nq), bf),
                dma(n_up), dma(n_up), dma(n_dn), dma(n_dn), dma(3), dma(3),
                dma(n_up), dma(n_up), dma(n_up), dma(n_up), dma(n_up), dma(n_up),
                dma(2), dma(2), dma(2), dma(2), dma(rows // TM),
            ],
            compiler_params=pltpu.CompilerParams(
                collective_id=0, has_side_effects=True, vmem_limit_bytes=67_000_000),
        )(x, w1, w2)
        return outs[0]

    act_spec = P(ROW_AXES, COL_AXES)
    wgt_spec = P("row", COL_AXES)
    return jax.shard_map(local_mlp, mesh=mesh, in_specs=(act_spec, wgt_spec, wgt_spec), out_specs=act_spec, check_vma=False)
```

time: 1220 us -> 645 us (0.53)
  waiting for transfers between devices: 1060 us -> 0 us
  Pallas kernels: 0 us -> 640 us
  matrix products: 147 us -> 0 us
  between operations: 13.1 us -> 0.01 us
    all_gather x4 -> x0, waiting for transfers between devices: 1060 us -> none  [the longest x1 345 us: local_mlp(): h_rows = lax.all_gather(hidden, COL_AXES, axis=1, tiled=True)]
    pallas_call x0 -> x1, Pallas kernels: none -> 640 us  [local_mlp(): pl.pallas_call(kernel, name='mlp', out_shape=(jax.ShapeDtypeStruct((rows,...]
    dot_general x2 -> x0, matrix products: 147 us -> none  [the longest x1 77.8 us: local_mlp(): pre_act = jnp.dot(x_rows, w_up_cols, preferred_element_type=jnp.float32)]
  transfers between devices with their start and end apart: 4 -> 0, of which waited for: 4 -> 0; matrix products, arithmetic and copies ran while one was open for 6% -> 0% of each run, Pallas kernels for 0% -> 0%
where the time goes in v1:
time: 645 us; the launch traced here: 644 us
  Pallas kernels  640 us (99%)
    pallas_call x1, Pallas kernels, local_mlp(): pl.pallas_call(kernel, name='mlp', out_shape=(jax.ShapeDtypeStruct((rows,...  640 us

profile of v1, /device:TPU:0, one launch (start us, length us, event | category | flops | bytes accessed | tf_op | source)
XLA Modules:
  0.0 644.4 jit_solution(5092729960491523007)
XLA Ops:
  0.0 639.7 %mlp.1 = (bf16[2048,1024]{1,0:T(8,128)(2,1)}, bf16[2048,3584]{1,0:T(8,128)(2,1)}, bf16[2,2,2048,3584]{3,2,1,0:T(8,128)(2,1)}) custom-call(bf16[2048,1024]{1,0:T(8,128)(2,1)} %x.1, bf16[2048,3584]{1,0:T(8,128)(2,1)} %w1.1, bf16[7168,1024]{1,0:T(8,128)(2,1)} %w2.1), custom_call_target="tpu_custom_call" | custom-call | tf_op jit(solution)/shard_map/mlp/pallas_call | solution.py:239
  639.7 4.6 copy.5

commit v2 on v0

v2 whole, which is shorter than its diff:
```python
import math

import jax
import jax.numpy as jnp
from jax import lax
from jax.experimental import pallas as pl
from jax.experimental.pallas import tpu as pltpu
from jax.sharding import PartitionSpec as P

ROW_AXES = ("dp", "row")
COL_AXES = ("co", "ci")
MESH = pl.DeviceIdType.MESH
T = 256
TN = 256
LAG_FWD = 2
LAG_DOWN = 3
SLOTS = 4
GELU_C = math.sqrt(2.0 / math.pi)


def gelu(p):
    return 0.5 * p * (1.0 + jnp.tanh(GELU_C * (p + 0.044715 * (p * p * p))))


def each(lo, hi, fn):
    def body(i, c):
        fn(i)
        return c

    lax.fori_loop(lo, hi, body, 0)


def kernel(x, w1, w2, y, xg, hg, yp, wv, w2v, xv, hv, hb, yf, yin, yo,
           s_xa, r_xa, s_xb, r_xb, s_xc, r_xc, s_xd, r_xd, s_xe, r_xe, s_xf, r_xf, s_xh, r_xh,
           s_w, r_w, s_l, s_hl, s_hf, r_hf, s_hm, r_hm, s_hw, r_hw, s_yf, r_yf, s_ld, s_yo):
    f32 = jnp.float32
    rows, kq = x.shape
    kh, fq = w1.shape
    nq = w2.shape[1]
    hc = fq // 2
    n = rows // T
    steps = 2 * n
    row, co, ci = lax.axis_index("row"), lax.axis_index("co"), lax.axis_index("ci")
    vert, far, mate = {"row": 1 - row}, {"co": 1 - co}, {"ci": 1 - ci}
    corner = {"row": 1 - row, "co": 1 - co}

    barrier = pltpu.get_barrier_semaphore()
    for dev in (vert, far, mate, corner):
        pl.semaphore_signal(barrier, inc=1, device_id=dev, device_id_type=MESH)
    pl.semaphore_wait(barrier, 4)

    def rdma(src, dst, send, recv, dev):
        return pltpu.make_async_remote_copy(
            src_ref=src, dst_ref=dst, send_sem=send, recv_sem=recv, device_id=dev, device_id_type=MESH)

    def tok(j):
        return pl.ds(pl.multiple_of(j * T, T), T)

    def half(c):
        return pl.ds(pl.multiple_of(c * hc, TN), hc)

    def xa(j):
        return rdma(x.at[tok(j)], xg.at[row, co, ci, tok(j)], s_xa.at[j], r_xa.at[j], far)

    def xb(j):
        return rdma(x.at[tok(j)], xg.at[row, co, ci, tok(j)], s_xb.at[j], r_xb.at[j], vert)

    def pass_on(r, c, j, send, recv, dev):
        blk = xg.at[r, c, ci, tok(j)]
        return rdma(blk, blk, send.at[j], recv.at[j], dev)

    def xc(j):
        return pass_on(row, 1 - co, j, s_xc, r_xc, vert)

    def xe(j):
        return pass_on(row, 1 - co, j, s_xe, r_xe, mate)

    def xf(j):
        return pass_on(1 - row, co, j, s_xf, r_xf, mate)

    def xh(j):
        return pass_on(1 - row, 1 - co, j, s_xh, r_xh, mate)

    xd = rdma(x, xg.at[row, co, ci], s_xd.at[0], r_xd.at[0], mate)

    w_x = rdma(w1.at[:, half(1 - co)], wv.at[row], s_w.at[0], r_w.at[row], {"row": co, "co": 1 - co})

    def w_y():
        return rdma(w1.at[:, half(co)], wv.at[row], s_w.at[1], r_w.at[row], vert)

    def w_here():
        return pltpu.make_async_copy(w1.at[:, half(co)], wv.at[row], s_l.at[0])

    def w_in(k):
        return rdma(w1.at[:, half(0)], wv.at[k], s_w.at[1], r_w.at[k], vert)

    w2_in = pltpu.make_async_copy(w2, w2v, s_l.at[1])

    def hf(i):
        return rdma(hv.at[lax.rem(i, SLOTS)], hg.at[co, ci, tok(i)], s_hf.at[i], r_hf.at[i], far)

    def hm(i):
        return rdma(hv.at[lax.rem(i, SLOTS)], hg.at[co, ci, tok(i)], s_hm.at[i], r_hm.at[i], mate)

    def hl(i):
        s = lax.rem(i, SLOTS)
        return pltpu.make_async_copy(hv.at[s], hg.at[co, ci, tok(i)], s_hl.at[s])

    def hw(i):
        blk = hg.at[1 - co, ci, tok(i)]
        return rdma(blk, blk, s_hw.at[i], r_hw.at[i], mate)

    def yc(j):
        return rdma(yf.at[j], yp.at[tok(j)], s_yf.at[j], r_yf.at[j], vert)

    def y_out(j):
        s = lax.rem(j, 2)
        return pltpu.make_async_copy(yo.at[s], y.at[tok(j)], s_yo.at[s])

    def relay(j):
        xc(j).start()
        xe(j).start()

    def meet(j):
        xb(j).wait_recv()
        xc(j).wait_recv()
        xf(j).start()
        xh(j).start()

    each(0, 2, lambda j: xa(j).start())
    each(0, 2, lambda j: xb(j).start())
    w_x.start()
    each(2, n, lambda j: xa(j).start())
    xd.start()
    w2_in.start()

    @pl.when(row == co)
    def _():
        w_here().start()

    def first(j):
        xa(j).wait_recv()
        relay(j)

    each(0, 2, first)

    @pl.when(row != co)
    def _():
        w_y().start()

    meet(0)

    @pl.when(row == co)
    def _():
        w_here().wait()
        w_in(1 - row).wait_recv()

    @pl.when(row != co)
    def _():
        w_in(0).wait_recv()
        w_in(1).wait_recv()

    w2_in.wait()

    def up(k):
        @pl.when(k < n)
        def _():
            xf(k).wait_recv()
            xh(k).wait_recv()
            ld = pltpu.make_async_copy(xg.at[1 - row, :, :, tok(k)], xv, s_ld.at[0])
            ld.start()
            ld.wait()

        @pl.when(k == n)
        def _():
            xd.wait_recv()

        @pl.when(k >= n)
        def _():
            j = k - n
            xe(j).wait_recv()
            lds = (
                pltpu.make_async_copy(xg.at[row, 1 - co, :, tok(j)], xv.at[1 - co], s_ld.at[0]),
                pltpu.make_async_copy(xg.at[row, co, 1 - ci, tok(j)], xv.at[co, 1 - ci], s_ld.at[1]),
                pltpu.make_async_copy(x.at[tok(j)], xv.at[co, ci], s_ld.at[2]),
            )
            for c in lds:
                c.start()
            for c in lds:
                c.wait()

        @pl.when(k >= SLOTS)
        def _():
            hf(k - SLOTS).wait_send()
            hm(k - SLOTS).wait_send()

        s = lax.rem(k, SLOTS)

        def tile(t):
            cols = pl.ds(pl.multiple_of(t * TN, TN), TN)
            p = None
            for a in range(2):
                for b in range(2):
                    d = jnp.dot(xv[a, b], wv[a, b * kq:(b + 1) * kq, cols], preferred_element_type=f32)
                    p = d if p is None else p + d
            hv[s, :, cols] = gelu(p).astype(jnp.bfloat16)

        each(0, hc // TN, tile)
        hf(k).start()
        hm(k).start()
        hl(k).start()

    def down(i):
        hl(i).wait()
        hm(i).wait_recv()
        hw(i).wait_recv()
        ld = pltpu.make_async_copy(hg.at[:, :, tok(i)], hb, s_ld.at[3])
        ld.start()
        other = i < n
        j = jnp.where(other, i, i - n)
        s = jnp.where(other, i, n)

        @pl.when(jnp.logical_not(other))
        def _():
            yc(j).wait_recv()
            part = pltpu.make_async_copy(yp.at[tok(j)], yin, s_ld.at[4])
            part.start()
            part.wait()

        ld.wait()

        def tile(t):
            cols = pl.ds(pl.multiple_of(t * TN, TN), TN)
            p = None
            for b in range(2):
                for a in range(2):
                    lo = b * fq + a * hc
                    d = jnp.dot(hb[a, b], w2v[lo:lo + hc, cols], preferred_element_type=f32)
                    p = d if p is None else p + d
            yf[s, :, cols] = p

        each(0, nq // TN, tile)

        @pl.when(other)
        def _():
            yc(j).start()

        @pl.when(jnp.logical_not(other))
        def _():
            @pl.when(j >= 2)
            def _():
                y_out(j - 2).wait()

            yo[lax.rem(j, 2)] = (yf[n] + yin[...]).astype(jnp.bfloat16)
            y_out(j).start()

    def step(k):
        @pl.when(k < steps)
        def _():
            up(k)

        @pl.when(k + 2 < n)
        def _():
            xa(k + 2).wait_recv()
            xb(k + 2).start()
            relay(k + 2)

        @pl.when(k + 1 < n)
        def _():
            meet(k + 1)

        @pl.when((k >= LAG_FWD) & (k < steps + LAG_FWD))
        def _():
            hf(k - LAG_FWD).wait_recv()
            hw(k - LAG_FWD).start()

        @pl.when(k >= LAG_DOWN)
        def _():
            down(k - LAG_DOWN)

    each(0, steps + LAG_DOWN, step)

    w_x.wait_send()

    @pl.when(row != co)
    def _():
        w_y().wait_send()

    xd.wait_send()

    def sent_x(j):
        for c in (xa, xb, xc, xe, xf, xh, yc):
            c(j).wait_send()

    each(0, n, sent_x)
    each(0, steps, lambda i: hw(i).wait_send())

    def sent_h(i):
        hf(i).wait_send()
        hm(i).wait_send()

    each(steps - SLOTS, steps, sent_h)
    each(n - 2, n, lambda j: y_out(j).wait())


def solution(mesh):
    def local_mlp(x, w1, w2):
        rows, kq = x.shape
        kh, fq = w1.shape
        fh, nq = w2.shape
        hc, n = fq // 2, rows // T
        bf, f32 = jnp.bfloat16, jnp.float32
        hbm = pl.BlockSpec(memory_space=pltpu.HBM)
        dma = lambda k: pltpu.SemaphoreType.DMA((k,))
        outs = pl.pallas_call(
            kernel,
            name="mlp",
            out_shape=(
                jax.ShapeDtypeStruct((rows, nq), bf),
                jax.ShapeDtypeStruct((2, 2, 2, rows, kq), bf),
                jax.ShapeDtypeStruct((2, 2, 2 * rows, hc), bf),
                jax.ShapeDtypeStruct((rows, nq), f32),
            ),
            in_specs=[hbm] * 3,
            out_specs=(hbm,) * 4,
            scratch_shapes=[
                pltpu.VMEM((2, kh, hc), bf),
                pltpu.VMEM((fh, nq), bf),
                pltpu.VMEM((2, 2, T, kq), bf),
                pltpu.VMEM((SLOTS, T, hc), bf),
                pltpu.VMEM((2, 2, T, hc), bf),
                pltpu.VMEM((n + 1, T, nq), f32),
                pltpu.VMEM((T, nq), f32),
                pltpu.VMEM((2, T, nq), bf),
                dma(n), dma(n), dma(n), dma(n), dma(n), dma(n), dma(1), dma(1),
                dma(n), dma(n), dma(n), dma(n), dma(n), dma(n),
                dma(2), dma(2), dma(2), dma(SLOTS),
                dma(2 * n), dma(2 * n), dma(2 * n), dma(2 * n), dma(2 * n), dma(2 * n),
                dma(n), dma(n), dma(5), dma(2),
            ],
            compiler_params=pltpu.CompilerParams(
                collective_id=0, has_side_effects=True, vmem_limit_bytes=67_000_000),
        )(x, w1, w2)
        return outs[0]

    act_spec = P(ROW_AXES, COL_AXES)
    wgt_spec = P("row", COL_AXES)
    return jax.shard_map(local_mlp, mesh=mesh, in_specs=(act_spec, wgt_spec, wgt_spec), out_specs=act_spec, check_vma=False)
```

time: 1220 us -> 609 us (0.50)
  waiting for transfers between devices: 1060 us -> 0 us
  Pallas kernels: 0 us -> 604 us
  matrix products: 147 us -> 0 us
  between operations: 13.1 us -> 0.01 us
    all_gather x4 -> x0, waiting for transfers between devices: 1060 us -> none  [the longest x1 345 us: local_mlp(): h_rows = lax.all_gather(hidden, COL_AXES, axis=1, tiled=True)]
    pallas_call x0 -> x1, Pallas kernels: none -> 604 us  [local_mlp(): pl.pallas_call(kernel, name='mlp', out_shape=(jax.ShapeDtypeStruct((rows,...]
    dot_general x2 -> x0, matrix products: 147 us -> none  [the longest x1 77.8 us: local_mlp(): pre_act = jnp.dot(x_rows, w_up_cols, preferred_element_type=jnp.float32)]
  transfers between devices with their start and end apart: 4 -> 0, of which waited for: 4 -> 0; matrix products, arithmetic and copies ran while one was open for 6% -> 0% of each run, Pallas kernels for 0% -> 0%
where the time goes in v2:
time: 609 us; the launch traced here: 608 us
  Pallas kernels  604 us (99%)
    pallas_call x1, Pallas kernels, local_mlp(): pl.pallas_call(kernel, name='mlp', out_shape=(jax.ShapeDtypeStruct((rows,...  604 us

profile of v2, /device:TPU:0, one launch (start us, length us, event | category | flops | bytes accessed | tf_op | source)
XLA Modules:
  0.0 608.3 jit_solution(5448910141034988369)
XLA Ops:
  0.0 603.6 %mlp.1 = (bf16[2048,1024]{1,0:T(8,128)(2,1)}, bf16[2,2,2,2048,1024]{4,3,2,1,0:T(8,128)(2,1)}, bf16[2,2,4096,1792]{3,2,1,0:T(8,128)(2,1)}, f32[2048,1024]{1,0:T(8,128)}) custom-call(bf16[2048,1024]{1,0:T(8,128)(2,1)} %x.1, bf16[2048,3584]{1,0:T(8,128)(2,1)} %w1.1, bf16[7168,1024]{1,0:T(8,128)(2,1)} %w2.1), custom_call_target="tpu_custom_call" | custom-call | tf_op jit(solution)/shard_map/mlp/pallas_call | solution.py:315
  603.7 4.6 copy.5

commit v3 on v2

--- a/solution.py
+++ b/solution.py
@@ -254,31 +254,78 @@
             yo[lax.rem(j, 2)] = (yf[n] + yin[...]).astype(jnp.bfloat16)
             y_out(j).start()
 
+    def bring(j):
+        xa(j).wait_recv()
+        xb(j).start()
+        relay(j)
+
     def step(k):
         @pl.when(k < steps)
         def _():
             up(k)
 
-        @pl.when(k + 2 < n)
-        def _():
-            xa(k + 2).wait_recv()
-            xb(k + 2).start()
-            relay(k + 2)
+        lo = 2 + k * (k + 1) // 2
+        each(jnp.minimum(lo, n), jnp.minimum(lo + k + 1, n), bring)
 
         @pl.when(k + 1 < n)
         def _():
             meet(k + 1)
 
-        @pl.when((k >= LAG_FWD) & (k < steps + LAG_FWD))
+        @pl.when(k >= LAG_DOWN)
+        def _():
+            down(k - LAG_DOWN)
+
+        @pl.when(k >= LAG_FWD)
         def _():
             hf(k - LAG_FWD).wait_recv()
             hw(k - LAG_FWD).start()
 
-        @pl.when(k >= LAG_DOWN)
-        def _():
-            down(k - LAG_DOWN)
-
-    each(0, steps + LAG_DOWN, step)
+    last = steps - 1
+    each(0, last + LAG_FWD, step)
+    each(last - 1, last, down)
+
+    def piece(src, dst, sem):
+        c = pltpu.make_async_copy(src, dst, s_ld.at[sem])
+        c.start()
+        c.wait()
+
+    def w2_rows(a, b):
+        return pl.ds(pl.multiple_of(b * fq + a * hc, TN), hc)
+
+    hl(last).wait()
+    hm(last).wait_recv()
+    piece(hg.at[co, :, tok(last)], hb.at[co], 0)
+    yc(n - 1).wait_recv()
+    piece(yp.at[tok(n - 1)], yin, 1)
+    y_out(n - 3).wait()
+
+    def near(t):
+        cols = pl.ds(pl.multiple_of(t * TN, TN), TN)
+        p = yin[:, cols]
+        for b in range(2):
+            p = p + jnp.dot(hb[co, b], w2v[w2_rows(co, b), cols], preferred_element_type=f32)
+        yin[:, cols] = p
+
+    each(0, nq // TN, near)
+    hf(last).wait_recv()
+    hw(last).start()
+    piece(hg.at[1 - co, ci, tok(last)], hb.at[1 - co, ci], 2)
+
+    def away(t):
+        cols = pl.ds(pl.multiple_of(t * TN, TN), TN)
+        yin[:, cols] += jnp.dot(hb[1 - co, ci], w2v[w2_rows(1 - co, ci), cols], preferred_element_type=f32)
+
+    each(0, nq // TN, away)
+    hw(last).wait_recv()
+    piece(hg.at[1 - co, 1 - ci, tok(last)], hb.at[1 - co, 1 - ci], 3)
+
+    def final(t):
+        cols = pl.ds(pl.multiple_of(t * TN, TN), TN)
+        d = jnp.dot(hb[1 - co, 1 - ci], w2v[w2_rows(1 - co, 1 - ci), cols], preferred_element_type=f32)
+        yo[(n - 1) % 2, :, cols] = (yin[:, cols] + d).astype(jnp.bfloat16)
+
+    each(0, nq // TN, final)
+    y_out(n - 1).start()
 
     w_x.wait_send()
 

time: 609 us -> 582 us (0.956)
  Pallas kernels: 604 us -> 576 us
    pallas_call x1, Pallas kernels: 604 us -> 576 us  [local_mlp(): pl.pallas_call(kernel, name='mlp', out_shape=(jax.ShapeDtypeStruct((rows,...]
where the time goes in v3:
time: 582 us; the launch traced here: 581 us
  Pallas kernels  576 us (99%)
    pallas_call x1, Pallas kernels, local_mlp(): pl.pallas_call(kernel, name='mlp', out_shape=(jax.ShapeDtypeStruct((rows,...  576 us

profile of v3, /device:TPU:0, one launch (start us, length us, event | category | flops | bytes accessed | tf_op | source)
XLA Modules:
  0.0 580.8 jit_solution(16030561117392443695)
XLA Ops:
  0.0 576.2 %mlp.1 = (bf16[2048,1024]{1,0:T(8,128)(2,1)}, bf16[2,2,2,2048,1024]{4,3,2,1,0:T(8,128)(2,1)}, bf16[2,2,4096,1792]{3,2,1,0:T(8,128)(2,1)}, f32[2048,1024]{1,0:T(8,128)}) custom-call(bf16[2048,1024]{1,0:T(8,128)(2,1)} %x.1, bf16[2048,3584]{1,0:T(8,128)(2,1)} %w1.1, bf16[7168,1024]{1,0:T(8,128)(2,1)} %w2.1), custom_call_target="tpu_custom_call" | custom-call | tf_op jit(solution)/shard_map/mlp/pallas_call | solution.py:362
  576.2 4.6 copy.5

commit v4 on v0

v4 whole, which is shorter than its diff:
```python
import math

import jax
import jax.numpy as jnp
from jax import lax
from jax.experimental import pallas as pl
from jax.experimental.pallas import tpu as pltpu
from jax.sharding import PartitionSpec as P

ROW_AXES = ("dp", "row")
COL_AXES = ("co", "ci")
MESH = pl.DeviceIdType.MESH
T = 256
TN = 256
SA = 2048
DIRECT = 4
EARLY = 2
LAG_FWD = 3
LAG_DOWN = 4
SLOTS = 5
GELU_C = math.sqrt(2.0 / math.pi)


def gelu(p):
    return 0.5 * p * (1.0 + jnp.tanh(GELU_C * (p + 0.044715 * (p * p * p))))


def each(lo, hi, fn):
    def body(i, c):
        fn(i)
        return c

    lax.fori_loop(lo, hi, body, 0)


def program(diag, x, w1, w2, y, xg, hga, hgb, yp, wv, w2v, xv, hv, hba, hbb, yf, yin, yo,
            s_of, s_ov, s_pv, s_qr, s_pm, s_qm, s_rm, r_p, r_q, r_r, r_pm, r_qm, r_rm, s_xd, r_xd,
            s_wt, r_wt, s_wc, r_wc, s_l, s_hl, s_hf, r_hf, s_hm, r_hm, s_hw, r_hw, s_yf, r_yf, s_ld, s_yo):
    f32 = jnp.float32
    rows, kq = x.shape
    kh, fq = w1.shape
    nq = w2.shape[1]
    sb = fq - SA
    n = rows // T
    steps = 2 * n
    last = steps - 1
    row, co, ci = lax.axis_index("row"), lax.axis_index("co"), lax.axis_index("ci")
    vert, far, mate = {"row": 1 - row}, {"co": 1 - co}, {"ci": 1 - ci}
    corner = {"row": 1 - row, "co": 1 - co}
    mine = SA if diag else sb
    hg_mine, hg_far = (hga, hgb) if diag else (hgb, hga)
    hb_mine, hb_far = (hba, hbb) if diag else (hbb, hba)

    def rdma(src, dst, send, recv, dev):
        return pltpu.make_async_remote_copy(
            src_ref=src, dst_ref=dst, send_sem=send, recv_sem=recv, device_id=dev, device_id_type=MESH)

    def tok(j):
        return pl.ds(pl.multiple_of(j * T, T), T)

    def cols(t):
        return pl.ds(pl.multiple_of(t * TN, TN), TN)

    def own(j, send, recv, dev):
        return rdma(x.at[tok(j)], xg.at[row, co, ci, tok(j)], send.at[j], recv.at[j], dev)

    def own_far(j):
        return own(j, s_of, r_p, far)

    def own_vert(j):
        return own(j, s_ov, r_q, vert)

    def pass_on(r, c, j, send, recv, dev):
        blk = xg.at[r, c, ci, tok(j)]
        return rdma(blk, blk, send.at[j], recv.at[j], dev)

    def p_vert(j):
        return pass_on(row, 1 - co, j, s_pv, r_r, vert)

    def q_far(j):
        return pass_on(1 - row, co, j, s_qr, r_r, far)

    def r_vert(j):
        return pass_on(1 - row, 1 - co, j, s_qr, r_p, vert)

    def p_mate(j):
        return pass_on(row, 1 - co, j, s_pm, r_pm, mate)

    def q_mate(j):
        return pass_on(1 - row, co, j, s_qm, r_qm, mate)

    def r_mate(j):
        return pass_on(1 - row, 1 - co, j, s_rm, r_rm, mate)

    def got(recv, j):
        own(j, s_of, recv, far).wait_recv()

    xd = rdma(x, xg.at[row, co, ci], s_xd.at[0], r_xd.at[0], mate)

    w_cross = rdma(w1.at[:, SA:], wv.at[row, :, :sb], s_wc.at[0], r_wc.at[row], far if diag else corner)

    def w_tile(t):
        return rdma(w1.at[:, cols(t)], wv.at[row, :, cols(t)], s_wt.at[t], r_wt.at[t], vert)

    def w_in(k):
        return rdma(w1.at[:, SA:], wv.at[k, :, :sb], s_wc.at[0], r_wc.at[k], far)

    w2_in = pltpu.make_async_copy(w2, w2v, s_l.at[1])

    def h_src(i):
        return hv.at[lax.rem(i, SLOTS), :, :mine]

    def hf(i):
        return rdma(h_src(i), hg_mine.at[ci, tok(i)], s_hf.at[i], r_hf.at[i], far)

    def hm(i):
        return rdma(h_src(i), hg_mine.at[ci, tok(i)], s_hm.at[i], r_hm.at[i], mate)

    def hl(i):
        return pltpu.make_async_copy(h_src(i), hg_mine.at[ci, tok(i)], s_hl.at[lax.rem(i, SLOTS)])

    def hw(i):
        blk = hg_far.at[ci, tok(i)]
        return rdma(blk, blk, s_hw.at[i], r_hw.at[i], mate)

    def hf_got(i):
        blk = hg_far.at[ci, tok(i)]
        rdma(blk, blk, s_hw.at[i], r_hf.at[i], far).wait_recv()

    def yc(j):
        return rdma(yf.at[j], yp.at[tok(j)], s_yf.at[j], r_yf.at[j], vert)

    def y_out(j):
        s = lax.rem(j, 2)
        return pltpu.make_async_copy(yo.at[s], y.at[tok(j)], s_yo.at[s])

    def bring(j):
        def through():
            got(r_p, j)
            own_vert(j).start()
            p_vert(j).start()
            p_mate(j).start()

        if diag:
            through()
        else:
            pl.when(j < DIRECT)(through)

            @pl.when(j >= DIRECT)
            def _():
                own_vert(j).start()
                got(r_q, j)
                q_far(j).start()

    def meet(j):
        if diag:
            got(r_q, j)
        else:
            @pl.when(j < DIRECT)
            def _():
                got(r_q, j)
        got(r_r, j)
        if diag:
            @pl.when(j >= DIRECT)
            def _():
                r_vert(j).start()
        q_mate(j).start()
        r_mate(j).start()

    def own_loads(j, s):
        return (
            pltpu.make_async_copy(xg.at[row, 1 - co, :, tok(j)], xv.at[s, 1 - co], s_ld.at[3 * s]),
            pltpu.make_async_copy(xg.at[row, co, 1 - ci, tok(j)], xv.at[s, co, 1 - ci], s_ld.at[3 * s + 1]),
            pltpu.make_async_copy(x.at[tok(j)], xv.at[s, co, ci], s_ld.at[3 * s + 2]),
        )

    def up_tile(xs, hs, t):
        p = None
        for a in range(2):
            for b in range(2):
                d = jnp.dot(xv[xs, a, b], wv[a, b * kq:(b + 1) * kq, cols(t)], preferred_element_type=f32)
                p = d if p is None else p + d
        hv[hs, :, cols(t)] = gelu(p).astype(jnp.bfloat16)

    def send_h(k):
        hf(k).start()
        hm(k).start()
        hl(k).start()

    def up(k):
        other = k < EARLY + n

        @pl.when(other)
        def _():
            j = k - EARLY
            got(r_qm, j)
            got(r_rm, j)
            ld = pltpu.make_async_copy(xg.at[1 - row, :, :, tok(j)], xv.at[0], s_ld.at[0])
            ld.start()
            ld.wait()

        @pl.when(jnp.logical_not(other))
        def _():
            j = k - n
            got(r_pm, j)
            for c in own_loads(j, 0):
                c.start()
            for c in own_loads(j, 0):
                c.wait()

        @pl.when(k >= SLOTS)
        def _():
            hf(k - SLOTS).wait_send()
            hm(k - SLOTS).wait_send()

        hs = lax.rem(k, SLOTS)
        each(0, mine // TN, lambda t: up_tile(0, hs, t))
        send_h(k)

    def w2_rows(first, b):
        lo = b * fq + (0 if first else SA)
        size = SA if first else sb
        return pl.ds(lo if isinstance(lo, int) else pl.multiple_of(lo, TN), size)

    def out(j, part):
        @pl.when(j >= 2)
        def _():
            y_out(j - 2).wait()

        yo[lax.rem(j, 2)] = (part + yin[...]).astype(jnp.bfloat16)
        y_out(j).start()

    def part_in(j):
        yc(j).wait_recv()
        c = pltpu.make_async_copy(yp.at[tok(j)], yin, s_ld.at[6])
        c.start()
        c.wait()

    def down(i):
        hl(i).wait()
        hm_got(i)
        hw(i).wait_recv()
        lda = pltpu.make_async_copy(hga.at[:, tok(i)], hba, s_ld.at[7])
        ldb = pltpu.make_async_copy(hgb.at[:, tok(i)], hbb, s_ld.at[8])
        lda.start()
        ldb.start()
        other = (i >= EARLY) & (i < EARLY + n)
        late = i >= EARLY + n
        s = jnp.where(i < EARLY, n + i, jnp.where(other, i - EARLY, n + EARLY))

        @pl.when(late)
        def _():
            part_in(i - n)

        lda.wait()
        ldb.wait()

        def tile(t):
            p = None
            for first, hb in ((True, hba), (False, hbb)):
                for b in range(2):
                    d = jnp.dot(hb[b], w2v[w2_rows(first, b), cols(t)], preferred_element_type=f32)
                    p = d if p is None else p + d
            yf[s, :, cols(t)] = p

        each(0, nq // TN, tile)

        @pl.when(other)
        def _():
            yc(i - EARLY).start()

        @pl.when(late)
        def _():
            out(i - n, yf[n + EARLY])

    def hm_got(i):
        blk = hg_mine.at[ci, tok(i)]
        rdma(blk, blk, s_hw.at[i], r_hm.at[i], mate).wait_recv()

    if diag:
        each(0, EARLY, lambda j: own_far(j).start())
        w_cross.start()
        each(EARLY, DIRECT, lambda j: own_far(j).start())
        here = pltpu.make_async_copy(w1.at[:, :SA], wv.at[row], s_l.at[0])
        here.start()
    else:
        each(0, SA // TN, lambda t: w_tile(t).start())
        each(0, EARLY, lambda j: own_far(j).start())
        w_cross.start()
        each(EARLY, n, lambda j: own_far(j).start())
    xd.start()
    w2_in.start()
    each(0, EARLY, bring)
    xd.wait_recv()
    for j in range(EARLY):
        got(r_pm, j)
        for c in own_loads(j, j):
            c.start()
    for j in range(EARLY):
        for c in own_loads(j, j):
            c.wait()
    if diag:
        here.wait()
    else:
        w_in(0).wait_recv()
        w_in(1).wait_recv()

    def first_tiles(t):
        if diag:
            rdma(w1.at[:, cols(t)], wv.at[1 - row, :, cols(t)], s_wt.at[t], r_wt.at[t], vert).wait_recv()
        for j in range(EARLY):
            up_tile(j, j, t)

    each(0, mine // TN, first_tiles)
    each(0, EARLY, send_h)
    w2_in.wait()
    each(EARLY, 2 * EARLY, bring)
    meet(0)

    def step(k):
        @pl.when(k < steps)
        def _():
            up(k)

        each(jnp.minimum(n, 2 * k), jnp.minimum(n, 2 * k + 2), bring)

        @pl.when(k - 1 < n)
        def _():
            meet(k - 1)

        if not diag:
            @pl.when((k >= n - 2 + DIRECT) & (k < 2 * n - 2))
            def _():
                got(r_p, k - (n - 2))
                p_mate(k - (n - 2)).start()

        @pl.when((k >= n + EARLY) & (k < n + 2 * EARLY))
        def _():
            j = k - n - EARLY
            part_in(j)
            out(j, yf[n + j])

        @pl.when(k >= LAG_DOWN)
        def _():
            down(k - LAG_DOWN)

        @pl.when(k >= LAG_FWD)
        def _():
            hf_got(k - LAG_FWD)
            hw(k - LAG_FWD).start()

    each(EARLY, last + LAG_FWD, step)
    each(last - 1, last, down)

    def piece(src, dst):
        c = pltpu.make_async_copy(src, dst, s_ld.at[7])
        c.start()
        c.wait()

    hl(last).wait()
    hm_got(last)
    piece(hg_mine.at[:, tok(last)], hb_mine)
    part_in(n - 1)
    y_out(n - 3).wait()

    def near(t):
        p = yin[:, cols(t)]
        for b in range(2):
            p = p + jnp.dot(hb_mine[b], w2v[w2_rows(diag, b), cols(t)], preferred_element_type=f32)
        yin[:, cols(t)] = p

    each(0, nq // TN, near)
    hf_got(last)
    hw(last).start()
    piece(hg_far.at[ci, tok(last)], hb_far.at[ci])

    def away(t):
        yin[:, cols(t)] += jnp.dot(hb_far[ci], w2v[w2_rows(not diag, ci), cols(t)], preferred_element_type=f32)

    each(0, nq // TN, away)
    hw(last).wait_recv()
    piece(hg_far.at[1 - ci, tok(last)], hb_far.at[1 - ci])

    def final(t):
        d = jnp.dot(hb_far[1 - ci], w2v[w2_rows(not diag, 1 - ci), cols(t)], preferred_element_type=f32)
        yo[(n - 1) % 2, :, cols(t)] = (yin[:, cols(t)] + d).astype(jnp.bfloat16)

    each(0, nq // TN, final)
    y_out(n - 1).start()

    w_cross.wait_send()
    xd.wait_send()
    if not diag:
        each(0, SA // TN, lambda t: w_tile(t).wait_send())
    each(0, DIRECT if diag else n, lambda j: own_far(j).wait_send())
    each(0, n if diag else DIRECT, lambda j: p_vert(j).wait_send())
    each(DIRECT, n, lambda j: (r_vert(j) if diag else q_far(j)).wait_send())

    def sent_x(j):
        for c in (own_vert, p_mate, q_mate, r_mate, yc):
            c(j).wait_send()

    each(0, n, sent_x)
    each(0, steps, lambda i: hw(i).wait_send())

    def sent_h(i):
        hf(i).wait_send()
        hm(i).wait_send()

    each(steps - SLOTS, steps, sent_h)
    each(n - 2, n, lambda j: y_out(j).wait())


def kernel(*refs):
    row, co, ci = lax.axis_index("row"), lax.axis_index("co"), lax.axis_index("ci")
    barrier = pltpu.get_barrier_semaphore()
    for dev in ({"row": 1 - row}, {"co": 1 - co}, {"ci": 1 - ci}, {"row": 1 - row, "co": 1 - co}):
        pl.semaphore_signal(barrier, inc=1, device_id=dev, device_id_type=MESH)
    pl.semaphore_wait(barrier, 4)

    @pl.when(row == co)
    def _():
        program(True, *refs)

    @pl.when(row != co)
    def _():
        program(False, *refs)


def solution(mesh):
    def local_mlp(x, w1, w2):
        rows, kq = x.shape
        kh, fq = w1.shape
        fh, nq = w2.shape
        sb, n = fq - SA, rows // T
        bf, f32 = jnp.bfloat16, jnp.float32
        hbm = pl.BlockSpec(memory_space=pltpu.HBM)
        dma = lambda k: pltpu.SemaphoreType.DMA((k,))
        outs = pl.pallas_call(
            kernel,
            name="mlp",
            out_shape=(
                jax.ShapeDtypeStruct((rows, nq), bf),
                jax.ShapeDtypeStruct((2, 2, 2, rows, kq), bf),
                jax.ShapeDtypeStruct((2, 2 * rows, SA), bf),
                jax.ShapeDtypeStruct((2, 2 * rows, sb), bf),
                jax.ShapeDtypeStruct((rows, nq), f32),
            ),
            in_specs=[hbm] * 3,
            out_specs=(hbm,) * 5,
            scratch_shapes=[
                pltpu.VMEM((2, kh, SA), bf),
                pltpu.VMEM((fh, nq), bf),
                pltpu.VMEM((EARLY, 2, 2, T, kq), bf),
                pltpu.VMEM((SLOTS, T, SA), bf),
                pltpu.VMEM((2, T, SA), bf),
                pltpu.VMEM((2, T, sb), bf),
                pltpu.VMEM((n + EARLY + 1, T, nq), f32),
                pltpu.VMEM((T, nq), f32),
                pltpu.VMEM((2, T, nq), bf),
                *[dma(n)] * 13, dma(1), dma(1),
                dma(SA // TN), dma(SA // TN), dma(1), dma(2), dma(2), dma(SLOTS),
                *[dma(2 * n)] * 6,
                dma(n), dma(n), dma(9), dma(2),
            ],
            compiler_params=pltpu.CompilerParams(
                collective_id=0, has_side_effects=True, vmem_limit_bytes=67_000_000),
        )(x, w1, w2)
        return outs[0]

    act_spec = P(ROW_AXES, COL_AXES)
    wgt_spec = P("row", COL_AXES)
    return jax.shard_map(local_mlp, mesh=mesh, in_specs=(act_spec, wgt_spec, wgt_spec), out_specs=act_spec, check_vma=False)
```

time: 1220 us -> 573 us (0.47)
  waiting for transfers between devices: 1060 us -> 0 us
  Pallas kernels: 0 us -> 558 us
  matrix products: 147 us -> 0 us
  between operations: 13.1 us -> 0.01 us
    all_gather x4 -> x0, waiting for transfers between devices: 1060 us -> none  [the longest x1 345 us: local_mlp(): h_rows = lax.all_gather(hidden, COL_AXES, axis=1, tiled=True)]
    pallas_call x0 -> x1, Pallas kernels: none -> 558 us  [local_mlp(): pl.pallas_call(kernel, name='mlp', out_shape=(jax.ShapeDtypeStruct((rows,...]
    dot_general x2 -> x0, matrix products: 147 us -> none  [the longest x1 77.8 us: local_mlp(): pre_act = jnp.dot(x_rows, w_up_cols, preferred_element_type=jnp.float32)]
  transfers between devices with their start and end apart: 4 -> 0, of which waited for: 4 -> 0; matrix products, arithmetic and copies ran while one was open for 6% -> 0% of each run, Pallas kernels for 0% -> 0%
where the time goes in v4:
time: 573 us; the launch traced here: 562 us
  Pallas kernels  558 us (97%)
    pallas_call x1, Pallas kernels, local_mlp(): pl.pallas_call(kernel, name='mlp', out_shape=(jax.ShapeDtypeStruct((rows,...  558 us

profile of v4, /device:TPU:0, one launch (start us, length us, event | category | flops | bytes accessed | tf_op | source)
XLA Modules:
  0.0 562.3 jit_solution(16501020801461366530)
XLA Ops:
  0.0 557.7 %mlp.1 = (bf16[2048,1024]{1,0:T(8,128)(2,1)}, bf16[2,2,2,2048,1024]{4,3,2,1,0:T(8,128)(2,1)}, bf16[2,4096,2048]{2,1,0:T(8,128)(2,1)}, bf16[2,4096,1536]{2,1,0:T(8,128)(2,1)}, f32[2048,1024]{1,0:T(8,128)}) custom-call(bf16[2048,1024]{1,0:T(8,128)(2,1)} %refs_0_.1, bf16[2048,3584]{1,0:T(8,128)(2,1)} %refs_1_.1, bf16[7168,1024]{1,0:T(8,128)(2,1)} %refs_2_.1), custom_call_target="tpu_custom_call" | custom-call | tf_op jit(solution)/shard_map/mlp/pallas_call | solution.py:439
  557.7 4.6 copy.5

commit v5 on v4

--- a/solution.py
+++ b/solution.py
@@ -15,6 +15,7 @@
 SA = 2048
 DIRECT = 4
 EARLY = 2
+Z = 1
 LAG_FWD = 3
 LAG_DOWN = 4
 SLOTS = 5
@@ -33,9 +34,9 @@
     lax.fori_loop(lo, hi, body, 0)
 
 
-def program(diag, x, w1, w2, y, xg, hga, hgb, yp, wv, w2v, xv, hv, hba, hbb, yf, yin, yo,
+def program(diag, x, w1, w2, y, xg, hga, hgb, yp, zp, wv, w2v, xv, hv, hba, hbb, yf, yin, yo, yz,
             s_of, s_ov, s_pv, s_qr, s_pm, s_qm, s_rm, r_p, r_q, r_r, r_pm, r_qm, r_rm, s_xd, r_xd,
-            s_wt, r_wt, s_wc, r_wc, s_l, s_hl, s_hf, r_hf, s_hm, r_hm, s_hw, r_hw, s_yf, r_yf, s_ld, s_yo):
+            s_wt, r_wt, s_wc, r_wc, s_l, s_hl, s_hf, r_hf, s_hm, r_hm, s_hw, r_hw, s_yf, r_yf, s_z, r_zp, r_z, s_ld, s_yo):
     f32 = jnp.float32
     rows, kq = x.shape
     kh, fq = w1.shape
@@ -130,6 +131,12 @@
     def yc(j):
         return rdma(yf.at[j], yp.at[tok(j)], s_yf.at[j], r_yf.at[j], vert)
 
+    def z_part(j):
+        return rdma(yf.at[n + j], zp.at[tok(j)], s_z.at[j], r_zp.at[j], vert)
+
+    def z_sum(j):
+        return rdma(yz.at[j], y.at[tok(j)], s_z.at[j], r_z.at[j], vert)
+
     def y_out(j):
         s = lax.rem(j, 2)
         return pltpu.make_async_copy(yo.at[s], y.at[tok(j)], s_yo.at[s])
@@ -223,16 +230,16 @@
         return pl.ds(lo if isinstance(lo, int) else pl.multiple_of(lo, TN), size)
 
     def out(j, part):
-        @pl.when(j >= 2)
+        @pl.when(j >= 2 + (0 if diag else Z))
         def _():
             y_out(j - 2).wait()
 
         yo[lax.rem(j, 2)] = (part + yin[...]).astype(jnp.bfloat16)
         y_out(j).start()
 
-    def part_in(j):
-        yc(j).wait_recv()
-        c = pltpu.make_async_copy(yp.at[tok(j)], yin, s_ld.at[6])
+    def part_in(j, copy=yc, ref=yp):
+        copy(j).wait_recv()
+        c = pltpu.make_async_copy(ref.at[tok(j)], yin, s_ld.at[6])
         c.start()
         c.wait()
 
@@ -265,7 +272,12 @@
 
         each(0, nq // TN, tile)
 
-        @pl.when(other)
+        if not diag:
+            @pl.when(i < Z)
+            def _():
+                z_part(i).start()
+
+        @pl.when(other & (i >= EARLY + (Z if diag else 0)))
         def _():
             yc(i - EARLY).start()
 
@@ -337,8 +349,21 @@
         @pl.when((k >= n + EARLY) & (k < n + 2 * EARLY))
         def _():
             j = k - n - EARLY
-            part_in(j)
-            out(j, yf[n + j])
+
+            def whole():
+                part_in(j)
+                out(j, yf[n + j])
+
+            if diag:
+                whole()
+
+                @pl.when(j < Z)
+                def _():
+                    part_in(j, z_part, zp)
+                    yz[j] = (yf[j] + yin[...]).astype(jnp.bfloat16)
+                    z_sum(j).start()
+            else:
+                pl.when(j >= Z)(whole)
 
         @pl.when(k >= LAG_DOWN)
         def _():
@@ -360,14 +385,14 @@
     hl(last).wait()
     hm_got(last)
     piece(hg_mine.at[:, tok(last)], hb_mine)
-    part_in(n - 1)
     y_out(n - 3).wait()
 
     def near(t):
-        p = yin[:, cols(t)]
+        p = None
         for b in range(2):
-            p = p + jnp.dot(hb_mine[b], w2v[w2_rows(diag, b), cols(t)], preferred_element_type=f32)
-        yin[:, cols(t)] = p
+            d = jnp.dot(hb_mine[b], w2v[w2_rows(diag, b), cols(t)], preferred_element_type=f32)
+            p = d if p is None else p + d
+        yf[n + EARLY, :, cols(t)] = p
 
     each(0, nq // TN, near)
     hf_got(last)
@@ -375,15 +400,17 @@
     piece(hg_far.at[ci, tok(last)], hb_far.at[ci])
 
     def away(t):
-        yin[:, cols(t)] += jnp.dot(hb_far[ci], w2v[w2_rows(not diag, ci), cols(t)], preferred_element_type=f32)
+        yf[n + EARLY, :, cols(t)] += jnp.dot(
+            hb_far[ci], w2v[w2_rows(not diag, ci), cols(t)], preferred_element_type=f32)
 
     each(0, nq // TN, away)
+    part_in(n - 1)
     hw(last).wait_recv()
     piece(hg_far.at[1 - ci, tok(last)], hb_far.at[1 - ci])
 
     def final(t):
         d = jnp.dot(hb_far[1 - ci], w2v[w2_rows(not diag, 1 - ci), cols(t)], preferred_element_type=f32)
-        yo[(n - 1) % 2, :, cols(t)] = (yin[:, cols(t)] + d).astype(jnp.bfloat16)
+        yo[(n - 1) % 2, :, cols(t)] = (yf[n + EARLY, :, cols(t)] + d + yin[:, cols(t)]).astype(jnp.bfloat16)
 
     each(0, nq // TN, final)
     y_out(n - 1).start()
@@ -397,10 +424,14 @@
     each(DIRECT, n, lambda j: (r_vert(j) if diag else q_far(j)).wait_send())
 
     def sent_x(j):
-        for c in (own_vert, p_mate, q_mate, r_mate, yc):
+        for c in (own_vert, p_mate, q_mate, r_mate):
             c(j).wait_send()
 
     each(0, n, sent_x)
+    each(Z if diag else 0, n, lambda j: yc(j).wait_send())
+    each(0, Z, lambda j: (z_sum if diag else z_part)(j).wait_send())
+    if not diag:
+        each(0, Z, lambda j: z_sum(j).wait_recv())
     each(0, steps, lambda i: hw(i).wait_send())
 
     def sent_h(i):
@@ -445,9 +476,10 @@
                 jax.ShapeDtypeStruct((2, 2 * rows, SA), bf),
                 jax.ShapeDtypeStruct((2, 2 * rows, sb), bf),
                 jax.ShapeDtypeStruct((rows, nq), f32),
+                jax.ShapeDtypeStruct((Z * T, nq), f32),
             ),
             in_specs=[hbm] * 3,
-            out_specs=(hbm,) * 5,
+            out_specs=(hbm,) * 6,
             scratch_shapes=[
                 pltpu.VMEM((2, kh, SA), bf),
                 pltpu.VMEM((fh, nq), bf),
@@ -458,10 +490,11 @@
                 pltpu.VMEM((n + EARLY + 1, T, nq), f32),
                 pltpu.VMEM((T, nq), f32),
                 pltpu.VMEM((2, T, nq), bf),
+                pltpu.VMEM((Z, T, nq), bf),
                 *[dma(n)] * 13, dma(1), dma(1),
                 dma(SA // TN), dma(SA // TN), dma(1), dma(2), dma(2), dma(SLOTS),
                 *[dma(2 * n)] * 6,
-                dma(n), dma(n), dma(9), dma(2),
+                dma(n), dma(n), dma(Z), dma(Z), dma(Z), dma(9), dma(2),
             ],
             compiler_params=pltpu.CompilerParams(
                 collective_id=0, has_side_effects=True, vmem_limit_bytes=67_000_000),

time: 573 us -> 562 us (0.981); the launches traced: 562 us -> 559 us
  no operation moved by 1% of the time
where the time goes in v5:
time: 562 us; the launch traced here: 559 us
  Pallas kernels  555 us (99%)
    pallas_call x1, Pallas kernels, local_mlp(): pl.pallas_call(kernel, name='mlp', out_shape=(jax.ShapeDtypeStruct((rows,...  555 us

profile of v5, /device:TPU:0, one launch (start us, length us, event | category | flops | bytes accessed | tf_op | source)
XLA Modules:
  0.0 559.4 jit_solution(11535806912765286826)
XLA Ops:
  0.0 554.8 %mlp.1 = (bf16[2048,1024]{1,0:T(8,128)(2,1)}, bf16[2,2,2,2048,1024]{4,3,2,1,0:T(8,128)(2,1)}, bf16[2,4096,2048]{2,1,0:T(8,128)(2,1)}, bf16[2,4096,1536]{2,1,0:T(...) custom-call(bf16[2048,1024]{1,0:T(8,128)(2,1)} %refs_0_.1, bf16[2048,3584]{1,0:T(8,128)(2,1)} %refs_1_.1, ...), custom_call_target="tpu_custom_call" | custom-call | tf_op jit(solution)/shard_map/mlp/pallas_call | solution.py:470
  554.8 4.6 copy.5

commit v6 on v5

--- a/solution.py
+++ b/solution.py
@@ -19,6 +19,8 @@
 LAG_FWD = 3
 LAG_DOWN = 4
 SLOTS = 5
+SUB = 2
+HOLD = 6
 GELU_C = math.sqrt(2.0 / math.pi)
 
 
@@ -34,9 +36,9 @@
     lax.fori_loop(lo, hi, body, 0)
 
 
-def program(diag, x, w1, w2, y, xg, hga, hgb, yp, zp, wv, w2v, xv, hv, hba, hbb, yf, yin, yo, yz,
+def program(diag, x, w1, w2, y, xg, hga, hgb, yp, zp, wv, w2v, xv, hv, hba, hbb, hz, yf, yin, yo, yz,
             s_of, s_ov, s_pv, s_qr, s_pm, s_qm, s_rm, r_p, r_q, r_r, r_pm, r_qm, r_rm, s_xd, r_xd,
-            s_wt, r_wt, s_wc, r_wc, s_l, s_hl, s_hf, r_hf, s_hm, r_hm, s_hw, r_hw, s_yf, r_yf, s_z, r_zp, r_z, s_ld, s_yo):
+            s_wt, r_wt, s_wc, r_wc, s_l, s_hl, s_hf, r_hf, s_hm, r_hm, s_hw, r_hw, s_yf, r_yf, s_z, r_zp, r_z, s_hz, r_hz, s_hy, r_hy, s_yl, s_ld, s_yo):
     f32 = jnp.float32
     rows, kq = x.shape
     kh, fq = w1.shape
@@ -124,6 +126,21 @@
         blk = hg_far.at[ci, tok(i)]
         return rdma(blk, blk, s_hw.at[i], r_hw.at[i], mate)
 
+    def sub(u):
+        return pl.ds(pl.multiple_of(u * (T // SUB), T // SUB), T // SUB)
+
+    def hz_far(u):
+        return rdma(hv.at[last % SLOTS, sub(u), :mine], hz.at[ci, sub(u), :mine], s_hz.at[u], r_hz.at[u], far)
+
+    def hz_blk(c, u):
+        return hz.at[c, sub(u), :fq - mine]
+
+    def hz_got(u):
+        rdma(hz_blk(ci, u), hz_blk(ci, u), s_hz.at[u], r_hz.at[u], far).wait_recv()
+
+    def hz_mate(u):
+        return rdma(hz_blk(ci, u), hz_blk(ci, u), s_hy.at[u], r_hy.at[u], mate)
+
     def hf_got(i):
         blk = hg_far.at[ci, tok(i)]
         rdma(blk, blk, s_hw.at[i], r_hf.at[i], far).wait_recv()
@@ -190,7 +207,14 @@
         hv[hs, :, cols(t)] = gelu(p).astype(jnp.bfloat16)
 
     def send_h(k):
-        hf(k).start()
+        @pl.when(k < last)
+        def _():
+            hf(k).start()
+
+        @pl.when(k == last)
+        def _():
+            each(0, SUB, lambda u: hz_far(u).start())
+
         hm(k).start()
         hl(k).start()
 
@@ -302,7 +326,16 @@
         each(EARLY, n, lambda j: own_far(j).start())
     xd.start()
     w2_in.start()
-    each(0, EARLY, bring)
+    if diag:
+        each(0, EARLY, lambda j: own_vert(j).start())
+
+        def near_only(j):
+            got(r_p, j)
+            p_mate(j).start()
+
+        each(0, EARLY, near_only)
+    else:
+        each(0, EARLY, bring)
     xd.wait_recv()
     for j in range(EARLY):
         got(r_pm, j)
@@ -320,6 +353,11 @@
     def first_tiles(t):
         if diag:
             rdma(w1.at[:, cols(t)], wv.at[1 - row, :, cols(t)], s_wt.at[t], r_wt.at[t], vert).wait_recv()
+
+            @pl.when(t == HOLD)
+            def _():
+                each(0, EARLY, lambda j: p_vert(j).start())
+
         for j in range(EARLY):
             up_tile(j, j, t)
 
@@ -395,25 +433,37 @@
         yf[n + EARLY, :, cols(t)] = p
 
     each(0, nq // TN, near)
-    hf_got(last)
-    hw(last).start()
-    piece(hg_far.at[ci, tok(last)], hb_far.at[ci])
-
-    def away(t):
-        yf[n + EARLY, :, cols(t)] += jnp.dot(
-            hb_far[ci], w2v[w2_rows(not diag, ci), cols(t)], preferred_element_type=f32)
-
-    each(0, nq // TN, away)
-    part_in(n - 1)
-    hw(last).wait_recv()
-    piece(hg_far.at[1 - ci, tok(last)], hb_far.at[1 - ci])
-
-    def final(t):
-        d = jnp.dot(hb_far[1 - ci], w2v[w2_rows(not diag, 1 - ci), cols(t)], preferred_element_type=f32)
-        yo[(n - 1) % 2, :, cols(t)] = (yf[n + EARLY, :, cols(t)] + d + yin[:, cols(t)]).astype(jnp.bfloat16)
-
-    each(0, nq // TN, final)
-    y_out(n - 1).start()
+    def y_last(u):
+        s = (n - 1) % 2
+        r = pl.ds(pl.multiple_of((n - 1) * T + u * (T // SUB), T // SUB), T // SUB)
+        return pltpu.make_async_copy(yo.at[s, sub(u)], y.at[r], s_yl.at[u])
+
+    def finish(u):
+        hz_got(u)
+        hz_mate(u).start()
+
+        def away(t):
+            yf[n + EARLY, sub(u), cols(t)] += jnp.dot(
+                hz[ci, sub(u), :fq - mine], w2v[w2_rows(not diag, ci), cols(t)], preferred_element_type=f32)
+
+        each(0, nq // TN, away)
+
+        @pl.when(u == 0)
+        def _():
+            part_in(n - 1)
+
+        hz_mate(u).wait_recv()
+
+        def final(t):
+            d = jnp.dot(hz[1 - ci, sub(u), :fq - mine], w2v[w2_rows(not diag, 1 - ci), cols(t)],
+                        preferred_element_type=f32)
+            yo[(n - 1) % 2, sub(u), cols(t)] = (
+                yf[n + EARLY, sub(u), cols(t)] + d + yin[sub(u), cols(t)]).astype(jnp.bfloat16)
+
+        each(0, nq // TN, final)
+        y_last(u).start()
+
+    each(0, SUB, finish)
 
     w_cross.wait_send()
     xd.wait_send()
@@ -432,14 +482,17 @@
     each(0, Z, lambda j: (z_sum if diag else z_part)(j).wait_send())
     if not diag:
         each(0, Z, lambda j: z_sum(j).wait_recv())
-    each(0, steps, lambda i: hw(i).wait_send())
-
-    def sent_h(i):
-        hf(i).wait_send()
-        hm(i).wait_send()
-
-    each(steps - SLOTS, steps, sent_h)
-    each(n - 2, n, lambda j: y_out(j).wait())
+    each(0, last, lambda i: hw(i).wait_send())
+    each(steps - SLOTS, last, lambda i: hf(i).wait_send())
+    each(steps - SLOTS, steps, lambda i: hm(i).wait_send())
+
+    def sent_last(u):
+        hz_far(u).wait_send()
+        hz_mate(u).wait_send()
+        y_last(u).wait()
+
+    each(0, SUB, sent_last)
+    y_out(n - 2).wait()
 
 
 def kernel(*refs):
@@ -487,6 +540,7 @@
                 pltpu.VMEM((SLOTS, T, SA), bf),
                 pltpu.VMEM((2, T, SA), bf),
                 pltpu.VMEM((2, T, sb), bf),
+                pltpu.VMEM((2, T, SA), bf),
                 pltpu.VMEM((n + EARLY + 1, T, nq), f32),
                 pltpu.VMEM((T, nq), f32),
                 pltpu.VMEM((2, T, nq), bf),
@@ -494,7 +548,7 @@
                 *[dma(n)] * 13, dma(1), dma(1),
                 dma(SA // TN), dma(SA // TN), dma(1), dma(2), dma(2), dma(SLOTS),
                 *[dma(2 * n)] * 6,
-                dma(n), dma(n), dma(Z), dma(Z), dma(Z), dma(9), dma(2),
+                dma(n), dma(n), dma(Z), dma(Z), dma(Z), *[dma(SUB)] * 5, dma(9), dma(2),
             ],
             compiler_params=pltpu.CompilerParams(
                 collective_id=0, has_side_effects=True, vmem_limit_bytes=67_000_000),

time: 562 us -> 558 us (level)
  no operation moved by 1% of the time
where the time goes in v6:
time: 558 us; the launch traced here: 557 us
  Pallas kernels  552 us (99%)
    pallas_call x1, Pallas kernels, local_mlp(): pl.pallas_call(kernel, name='mlp', out_shape=(jax.ShapeDtypeStruct((rows,...  552 us

profile of v6, /device:TPU:0, one launch (start us, length us, event | category | flops | bytes accessed | tf_op | source)
XLA Modules:
  0.0 556.9 jit_solution(17123293882064634334)
XLA Ops:
  0.0 552.3 %mlp.1 = (bf16[2048,1024]{1,0:T(8,128)(2,1)}, bf16[2,2,2,2048,1024]{4,3,2,1,0:T(8,128)(2,1)}, bf16[2,4096,2048]{2,1,0:T(8,128)(2,1)}, bf16[2,4096,1536]{2,1,0:T(...) custom-call(bf16[2048,1024]{1,0:T(8,128)(2,1)} %refs_0_.1, bf16[2048,3584]{1,0:T(8,128)(2,1)} %refs_1_.1, ...), custom_call_target="tpu_custom_call" | custom-call | tf_op jit(solution)/shard_map/mlp/pallas_call | solution.py:523
  552.3 4.6 copy.5

commit v7 on v6

--- a/solution.py
+++ b/solution.py
@@ -36,7 +36,7 @@
     lax.fori_loop(lo, hi, body, 0)
 
 
-def program(diag, x, w1, w2, y, xg, hga, hgb, yp, zp, wv, w2v, xv, hv, hba, hbb, hz, yf, yin, yo, yz,
+def program(diag, x, w1, w2, y, yl, xg, hga, hgb, yp, zp, wv, w2v, xv, hv, hba, hbb, hz, yf, yin, yo, yz,
             s_of, s_ov, s_pv, s_qr, s_pm, s_qm, s_rm, r_p, r_q, r_r, r_pm, r_qm, r_rm, s_xd, r_xd,
             s_wt, r_wt, s_wc, r_wc, s_l, s_hl, s_hf, r_hf, s_hm, r_hm, s_hw, r_hw, s_yf, r_yf, s_z, r_zp, r_z, s_hz, r_hz, s_hy, r_hy, s_yl, s_ld, s_yo):
     f32 = jnp.float32
@@ -62,7 +62,7 @@
         return pl.ds(pl.multiple_of(j * T, T), T)
 
     def cols(t):
-        return pl.ds(pl.multiple_of(t * TN, TN), TN)
+        return pl.ds(t * TN if isinstance(t, int) else pl.multiple_of(t * TN, TN), TN)
 
     def own(j, send, recv, dev):
         return rdma(x.at[tok(j)], xg.at[row, co, ci, tok(j)], send.at[j], recv.at[j], dev)
@@ -320,9 +320,9 @@
         here = pltpu.make_async_copy(w1.at[:, :SA], wv.at[row], s_l.at[0])
         here.start()
     else:
-        each(0, SA // TN, lambda t: w_tile(t).start())
         each(0, EARLY, lambda j: own_far(j).start())
         w_cross.start()
+        each(0, SA // TN, lambda t: w_tile(t).start())
         each(EARLY, n, lambda j: own_far(j).start())
     xd.start()
     w2_in.start()
@@ -435,8 +435,7 @@
     each(0, nq // TN, near)
     def y_last(u):
         s = (n - 1) % 2
-        r = pl.ds(pl.multiple_of((n - 1) * T + u * (T // SUB), T // SUB), T // SUB)
-        return pltpu.make_async_copy(yo.at[s, sub(u)], y.at[r], s_yl.at[u])
+        return pltpu.make_async_copy(yo.at[s, sub(u)], yl.at[sub(u)], s_yl.at[u])
 
     def finish(u):
         hz_got(u)
@@ -446,7 +445,8 @@
             yf[n + EARLY, sub(u), cols(t)] += jnp.dot(
                 hz[ci, sub(u), :fq - mine], w2v[w2_rows(not diag, ci), cols(t)], preferred_element_type=f32)
 
-        each(0, nq // TN, away)
+        for t in range(nq // TN):
+            away(t)
 
         @pl.when(u == 0)
         def _():
@@ -460,7 +460,8 @@
             yo[(n - 1) % 2, sub(u), cols(t)] = (
                 yf[n + EARLY, sub(u), cols(t)] + d + yin[sub(u), cols(t)]).astype(jnp.bfloat16)
 
-        each(0, nq // TN, final)
+        for t in range(nq // TN):
+            final(t)
         y_last(u).start()
 
     each(0, SUB, finish)
@@ -525,6 +526,7 @@
             name="mlp",
             out_shape=(
                 jax.ShapeDtypeStruct((rows, nq), bf),
+                jax.ShapeDtypeStruct((T, nq), bf),
                 jax.ShapeDtypeStruct((2, 2, 2, rows, kq), bf),
                 jax.ShapeDtypeStruct((2, 2 * rows, SA), bf),
                 jax.ShapeDtypeStruct((2, 2 * rows, sb), bf),
@@ -532,7 +534,7 @@
                 jax.ShapeDtypeStruct((Z * T, nq), f32),
             ),
             in_specs=[hbm] * 3,
-            out_specs=(hbm,) * 6,
+            out_specs=(hbm,) * 7,
             scratch_shapes=[
                 pltpu.VMEM((2, kh, SA), bf),
                 pltpu.VMEM((fh, nq), bf),
@@ -553,7 +555,8 @@
             compiler_params=pltpu.CompilerParams(
                 collective_id=0, has_side_effects=True, vmem_limit_bytes=67_000_000),
         )(x, w1, w2)
-        return outs[0]
+        late = lax.broadcasted_iota(jnp.int32, (rows // T, T, nq), 0) == rows // T - 1
+        return jnp.where(late, outs[1][None], outs[0].reshape(rows // T, T, nq)).reshape(rows, nq)
 
     act_spec = P(ROW_AXES, COL_AXES)
     wgt_spec = P("row", COL_AXES)

time: 558 us -> 556 us (level)
  no operation moved by 1% of the time
where the time goes in v7:
time: 556 us; the launch traced here: 554 us
  Pallas kernels  550 us (99%)
    pallas_call x1, Pallas kernels, local_mlp(): pl.pallas_call(kernel, name='mlp', out_shape=(jax.ShapeDtypeStruct((rows,...  550 us

profile of v7, /device:TPU:0, one launch (start us, length us, event | category | flops | bytes accessed | tf_op | source)
XLA Modules:
  0.0 554.5 jit_solution(11583684272004342956)
XLA Ops:
  0.0 550.4 %mlp.1 = (bf16[2048,1024]{1,0:T(8,128)(2,1)}, bf16[256,1024]{1,0:T(8,128)(2,1)}, bf16[2,2,2,2048,1024]{4,3,2,1,0:T(8,128)(2,1)}, bf16[2,4096,2048]{2,1,0:T(8,128...) custom-call(bf16[2048,1024]{1,0:T(8,128)(2,1)} %refs_0_.1, ...), custom_call_target="tpu_custom_call" | custom-call | tf_op jit(solution)/shard_map/mlp/pallas_call | solution.py:524
  550.4 0.1 iota.11
  550.5 4.0 bitcast_select_fusion
  (2 shorter events, 0.0 us)

commit v8 on v7

--- a/solution.py
+++ b/solution.py
@@ -464,8 +464,6 @@
             final(t)
         y_last(u).start()
 
-    each(0, SUB, finish)
-
     w_cross.wait_send()
     xd.wait_send()
     if not diag:
@@ -479,13 +477,19 @@
             c(j).wait_send()
 
     each(0, n, sent_x)
-    each(Z if diag else 0, n, lambda j: yc(j).wait_send())
+    each(Z if diag else 0, n - 1, lambda j: yc(j).wait_send())
     each(0, Z, lambda j: (z_sum if diag else z_part)(j).wait_send())
     if not diag:
         each(0, Z, lambda j: z_sum(j).wait_recv())
-    each(0, last, lambda i: hw(i).wait_send())
-    each(steps - SLOTS, last, lambda i: hf(i).wait_send())
-    each(steps - SLOTS, steps, lambda i: hm(i).wait_send())
+    each(0, last - 1, lambda i: hw(i).wait_send())
+    each(steps - SLOTS, last - 1, lambda i: hf(i).wait_send())
+    each(steps - SLOTS, last, lambda i: hm(i).wait_send())
+
+    each(0, SUB, finish)
+    yc(n - 1).wait_send()
+    hw(last - 1).wait_send()
+    hf(last - 1).wait_send()
+    hm(last).wait_send()
 
     def sent_last(u):
         hz_far(u).wait_send()

time: 556 us -> 556 us (level)
  no operation moved by 1% of the time
where the time goes in v8:
time: 556 us; the launch traced here: 555 us
  Pallas kernels  551 us (99%)
    pallas_call x1, Pallas kernels, local_mlp(): pl.pallas_call(kernel, name='mlp', out_shape=(jax.ShapeDtypeStruct((rows,...  551 us

profile of v8, /device:TPU:0, one launch (start us, length us, event | category | flops | bytes accessed | tf_op | source)
XLA Modules:
  0.0 554.8 jit_solution(7927582837981631096)
XLA Ops:
  0.0 550.7 %mlp.1 = (bf16[2048,1024]{1,0:T(8,128)(2,1)}, bf16[256,1024]{1,0:T(8,128)(2,1)}, bf16[2,2,2,2048,1024]{4,3,2,1,0:T(8,128)(2,1)}, bf16[2,4096,2048]{2,1,0:T(8,128...) custom-call(bf16[2048,1024]{1,0:T(8,128)(2,1)} %refs_0_.1, ...), custom_call_target="tpu_custom_call" | custom-call | tf_op jit(solution)/shard_map/mlp/pallas_call | solution.py:528
  550.7 0.1 iota.11
  550.8 4.0 bitcast_select_fusion
  (2 shorter events, 0.0 us)
